TPU v7x, 32 devices: a whole 2x2x4 slice. The times are simulated.
32 devices in a mesh: group: 2 (over y), sample: 16 (over z, x, core).
Axes of the slice: x: 2, y: 2, z: 4, core: 2. Of those that a mesh axis runs over, the one named last changes fastest.
Arguments:
- patches: bfloat16 [16, 256, 588], P('group', 'sample'), parts along dimension 0, may hold values from -6 to 6
- patch_weight: bfloat16 [16, 588, 1280], P('sample'), may hold values from -0.25 to 0.25
- cls_token: bfloat16 [16, 1280], P('sample'), may hold values from -6 to 6
- pos_embed: bfloat16 [16, 257, 1280], P('sample'), may hold values from -3 to 3
- ln1_gain: float32 [16, 1280], P('sample'), may hold values from 0.5 to 1.5
- ln1_bias: float32 [16, 1280], P('sample'), may hold values from -2 to 2
- w_query: bfloat16 [16, 1280, 640], P('sample'), may hold values from -8 to 8
- w_key: bfloat16 [16, 1280, 640], P('sample'), may hold values from -2 to 2
- w_value: bfloat16 [16, 1280, 640], P('sample'), may hold values from -0.15625 to 0.15625
- w_out: bfloat16 [16, 640, 1280], P('sample'), may hold values from -1 to 1
- lnf_gain: float32 [16, 1280], P('sample'), may hold values from 0.5 to 1.5
- lnf_bias: float32 [16, 1280], P('sample'), may hold values from -2 to 2
- head_w: bfloat16 [16, 1280, 1000], P('sample'), may hold values from -0.875 to 0.875
- head_bias: float32 [16, 1000], P('sample'), may hold values from -6 to 290
Outputs:
- predictive: float32 [16, 1000], P('group'), parts along dimension 0
There are 2 independent parts, one for each index of `group`. A program takes and returns all parts, laid end to end along the dimension named above; an argument that names none is the same for every part. Nothing has to cross between parts.
All inputs are finite; a program needn't handle non-finite values.
Results may differ from a plain program's by a relative error of at most 0.0023.
Values may be sent and summed in bfloat16 or wider, within the bound.
A program may use at most 64 MiB of HBM per device.

v0:
```python
import math

import jax
import jax.numpy as jnp
from jax import lax
from jax.sharding import PartitionSpec as P

HEAD_DIM = 80


epsilon = 1e-06


def combined_all(part, axis, combine):
    gathered = jax.tree.map(lambda a: lax.all_gather(a, axis), part)

    def take(source):
        return jax.tree.map(lambda a: lax.dynamic_index_in_dim(a, source, 0, False), gathered)

    return lax.fori_loop(
        1, lax.axis_size(axis), lambda source, state: combine(state, take(source)), take(0)
    )


def layer_norm(values, gain, shift):
    center = values - jnp.mean(values, axis=-1, keepdims=True)
    spread = jnp.mean(center * center, axis=-1, keepdims=True)
    return center * lax.rsqrt(spread + epsilon) * gain + shift


def shards(
    patches,
    patch_weight,
    cls_token,
    pos_embed,
    ln1_gain,
    ln1_bias,
    w_query,
    w_key,
    w_value,
    w_out,
    lnf_gain,
    lnf_bias,
    head_w,
    head_bias,
):
    embed_weight = patch_weight[0]
    position = pos_embed[0]
    gain_first = ln1_gain[0]
    bias_first = ln1_bias[0]
    query_weight = w_query[0]
    pair_weight = jnp.concatenate([w_key[0], w_value[0]], axis=1)
    out_weight = w_out[0]
    width = embed_weight.shape[1]
    inner = query_weight.shape[1]
    head_count = inner // HEAD_DIM
    leading = cls_token[0].astype(jnp.float32) + position[0].astype(jnp.float32)
    lead_norm = layer_norm(leading, gain_first, bias_first).astype(jnp.bfloat16)
    lead_pair = jnp.dot(lead_norm[None], pair_weight, preferred_element_type=jnp.float32).astype(
        jnp.bfloat16
    )
    query = jnp.dot(lead_norm[None], query_weight, preferred_element_type=jnp.float32).astype(
        jnp.bfloat16
    )
    query = query.reshape(head_count, HEAD_DIM)
    portion = lax.all_gather(patches, "sample", axis=1, tiled=True)
    image_count = portion.shape[0]
    row_count = portion.shape[1]
    flat = portion.reshape(-1, portion.shape[2])
    tokens = jnp.dot(flat, embed_weight, preferred_element_type=jnp.float32).reshape(
        image_count, row_count, width
    )
    placed = lax.dynamic_slice_in_dim(position, 1, row_count, 0)
    tokens = tokens + placed.astype(jnp.float32)[None]
    normed = layer_norm(tokens, gain_first, bias_first).astype(jnp.bfloat16)
    paired = jnp.dot(normed.reshape(-1, width), pair_weight, preferred_element_type=jnp.float32)
    key_values = paired.astype(jnp.bfloat16).reshape(image_count, row_count, 2 * inner)
    image_count = key_values.shape[0]
    lead_rows = jnp.broadcast_to(lead_pair[None], (image_count, 1, 2 * inner))
    full_rows = jnp.concatenate([lead_rows, key_values], axis=1)
    key_rows = full_rows[:, :, :inner].reshape(image_count, -1, head_count, HEAD_DIM)
    value_rows = full_rows[:, :, inner:].reshape(image_count, -1, head_count, HEAD_DIM)
    scores = jnp.einsum(
        "hd,ithd->iht", query, key_rows, preferred_element_type=jnp.float32
    ) / math.sqrt(HEAD_DIM)
    attention = jax.nn.softmax(scores, axis=-1).astype(jnp.bfloat16)
    mixed = jnp.einsum("iht,ithd->ihd", attention, value_rows, preferred_element_type=jnp.float32)
    mixed = mixed.astype(jnp.bfloat16).reshape(image_count, inner)
    hidden = leading[None] + jnp.dot(mixed, out_weight, preferred_element_type=jnp.float32)
    final = layer_norm(hidden, lnf_gain[0], lnf_bias[0]).astype(jnp.bfloat16)
    logits = jnp.dot(final, head_w[0], preferred_element_type=jnp.float32) + head_bias[0]
    logp = jax.nn.log_softmax(logits, axis=-1)
    count = lax.axis_size("sample")

    def combine(earlier, later):
        highest = jnp.maximum(earlier[0], later[0])
        summed = earlier[1] * jnp.exp(earlier[0] - highest) + later[1] * jnp.exp(later[0] - highest)
        return (highest, summed)

    peak, total = combined_all((logp, jnp.ones_like(logp)), "sample", combine)
    return peak + jnp.log(total) - math.log(count)


def solution(mesh):
    placed = (
        P("group", "sample", None),
        P("sample", None, None),
        P("sample", None),
        P("sample", None, None),
        P("sample", None),
        P("sample", None),
        P("sample", None, None),
        P("sample", None, None),
        P("sample", None, None),
        P("sample", None, None),
        P("sample", None),
        P("sample", None),
        P("sample", None, None),
        P("sample", None),
    )
    return jax.shard_map(
        shards, mesh=mesh, in_specs=placed, out_specs=P("group", None), check_vma=False
    )
```

profile of v0, /device:TPU:0, one launch (start us, length us, event | category | flops | bytes accessed | tf_op | source)
XLA Modules:
  0.0 138.1 jit_solution(11459945075896867940)
XLA Ops:
  6.5 0.0 copy-start
  6.5 0.0 copy-start.2
  6.5 0.0 all-gather.3.cloned.1.call-start
  6.5 0.7 all-gather.3.cloned.1.call-update
  7.3 0.8 reduce.4
  8.0 0.7 reduce.5
  8.7 0.7 convert_reduce_fusion
  9.5 0.8 fusion.42
  10.3 0.6 fusion.43
  11.5 0.6 multiply_reduce_fusion.2
  12.8 1.8 %fusion.23 = bf16[640]{0:T(1024)(128)(2,1)S(1)} fusion(bf16[1,1280,640]{2,1,0:T(8,128)(2,1)} %param.22, f32[1,1280]{1,0:T(1,128)} %param.21, f32[1,1280]{1,0:T(1,128)} %param.20, f32[]{:T(128)S(6)} %rsqrt.20, f32[]{:T(128)S(6)} %div.34, bf16[1,257,1280]{2,1,0:T(8,128)(2,1)} %param.19, bf16[1,1280]{1,0:T(2,128)(2,1)} %param.18), kind=kOutput, calls=%fused_computation.33 | convolution fusion | flops 1648640 | bytes 1660168 | tf_op jit(solution)/shard_map/dot_general | solution.py:62
  14.7 0.1 reshape.123
  14.7 0.7 reduce.7
  15.5 0.7 reduce.8
  16.2 2.6 %fusion.26 = bf16[1280]{0:T(1024)(128)(2,1)S(1)} fusion(bf16[1280,640]{1,0:T(8,128)(2,1)} %bitcast.90, bf16[1280,640]{1,0:T(8,128)(2,1)} %bitcast.92, f32[1,1280]{1,0:T(1,128)} %param.21, f32[1,1280]{1,0:T(1,128)} %param.20, f32[]{:T(128)S(6)} %rsqrt.20, f32[]{:T(128)S(6)} %div.34, bf16[1,257,1280]{2,1,0:T(8,128)(2,1)} %param.19, bf16[1,1280]{1,0:T(2,128)(2,1)} %param.18), kind=kOutput, calls=%fused_computation.34 | convolution fusion | flops 9840640 | bytes 3299848 | tf_op jit(solution)/shard_map/dot_general | solution.py:59
  18.7 0.0 copy-done.2
  18.7 1.2 bitcast_convert_fusion
  20.0 35.9 %all-gather.3.cloned.1.call-done = bf16[8,256,588]{2,1,0:T(8,128)(2,1)} async-done(((bf16[8,16,588]{2,1,0:T(8,128)(2,1)}), bf16[8,256,588]{2,1,0:T(8,128)(2,1)}) %all-gather.3.cloned.1.call-update) | async-done | bytes 2408464 | tf_op jit(solution)/shard_map/all_gather | solution.py:66
  55.9 0.0 copy-start.1
  55.9 7.3 %add_reduce_fusion = (f32[8,256]{1,0:T(8,128)S(1)}, f32[8,256,1280]{2,1,0:T(8,128)S(1)}) fusion(f32[256,1280]{1,0:T(8,128)} %bitcast_convert_fusion, bf16[8,256,588]{2,1,0:T(8,128)(2,1)} %all-gather.3.cloned.1.call-done, bf16[1,588,1280]{2,1,0:T(8,128)(2,1)} %param.17), kind=kOutput, calls=%fused_computation.9 | convolution fusion | flops 3088054272 | bytes 15718400 | tf_op jit(solution)/shard_map/dot_general | solution.py:70
  63.2 0.0 copy-done.1
  63.2 1.6 %multiply_reduce_fusion = f32[8,256]{1,0:T(8,128)S(1)} fusion(f32[8,256,1280]{2,1,0:T(8,128)S(1)} %get-tuple-element.161, f32[8,256]{1,0:T(8,128)S(1)} %broadcast_multiply_fusion, f32[256,1280]{1,0:T(8,128)S(1)} %copy-done.1), kind=kLoop, calls=%fused_computation.8 | loop fusion | flops 10483712 | bytes 11812864 | tf_op jit(solution)/shard_map/reduce_sum | solution.py:27
  64.9 0.0 copy-start.4
  64.9 0.0 copy-start.5
  64.9 2.5 %add_convert_fusion = bf16[8,256,1280]{2,1,0:T(8,128)(2,1)S(1)} fusion(f32[8,256,1280]{2,1,0:T(8,128)S(1)} %get-tuple-element.161, f32[1280]{0:T(1024)S(1)} %reduce.5, f32[1280]{0:T(1024)S(1)} %reduce.4, f32[8,256]{1,0:T(8,128)S(1)} %add_rsqrt_fusion, f32[8,256]{1,0:T(8,128)S(1)} %broadcast_multiply_fusion, f32[256,1280]{1,0:T(8,128)S(1)} %copy-done.1), kind=kLoop, calls=%fused_computation.7 | loop fusion | flops 15728640 | bytes 17065984 | tf_op jit(solution)/shard_map/convert_element_type | solution.py:75
  67.4 0.0 copy-done.4
  67.4 0.0 copy-done.5
  67.4 7.2 %convolution_convert_fusion = bf16[2048,1280]{1,0:T(8,128)(2,1)S(1)} fusion(bf16[2048,1280]{1,0:T(8,128)(2,1)S(1)} %bitcast.84, bf16[1280,640]{1,0:T(8,128)(2,1)S(1)} %bitcast.91, bf16[1280,640]{1,0:T(8,128)(2,1)S(1)} %bitcast.93), kind=kOutput, calls=%fused_computation.10 | convolution fusion | flops 6720061440 | bytes 13762560 | tf_op jit(solution)/shard_map/dot_general | solution.py:76
  74.7 2.9 %copy.16 = bf16[8,256,1280]{2,0,1:T(8,128)(2,1)S(1)} copy(bf16[8,256,1280]{2,1,0:T(8,128)(2,1)S(1)} %bitcast.85) | data formatting | bytes 10485760 | tf_op jit(solution)/shard_map/reshape | solution.py:77
  77.6 2.6 %fusion.6 = (bf16[8,257,640]{2,0,1:T(8,128)(2,1)}, bf16[8,257,640]{2,0,1:T(8,128)(2,1)}) fusion(bf16[8,1,1280]{2,0,1:T(8,128)(2,1)S(1)} %broadcast_in_dim.4, bf16[8,256,1280]{2,0,1:T(8,128)(2,1)S(1)} %copy.16), kind=kLoop, calls=%fused_computation.16 | loop fusion | flops 10526720 | bytes 10526720 | tf_op jit(solution)/shard_map/concatenate | solution.py:80
  80.2 7.9 %reshape.100 = bf16[8,257,8,80]{3,2,0,1:T(8,128)(2,1)} reshape(bf16[8,257,640]{2,0,1:T(8,128)(2,1)} %get-tuple-element.158) | data formatting | bytes 5263360 | tf_op jit(solution)/shard_map/reshape | solution.py:81
  88.1 8.3 %fusion.4 = f32[8,1,8,257]{3,1,2,0:T(1,128)S(1)} fusion(bf16[8,80,1,1]{1,2,3,0:T(2,128)(2,1)S(1)} %reshape.123, bf16[8,257,8,80]{3,2,0,1:T(8,128)(2,1)} %reshape.100), kind=kOutput, calls=%fused_computation.13 | convolution fusion | flops 2631680 | bytes 2698752 | tf_op jit(solution)/shard_map/hd,ithd->iht/dot_general | solution.py:83
  96.4 0.2 fusion.19
  96.6 5.7 %copy.23 = bf16[8,257,640]{1,2,0:T(8,128)(2,1)} copy(bf16[8,257,640]{2,0,1:T(8,128)(2,1)} %get-tuple-element.159) | data formatting | bytes 5263360 | tf_op jit(solution)/shard_map/reshape | solution.py:82
  102.3 0.0 copy-start.3
  102.3 3.6 %fusion.28 = f32[8,8,1,80]{3,2,1,0:T(1,128)S(1)} fusion(bf16[8,257,8,80]{1,3,2,0:T(8,128)(2,1)} %bitcast.86, bf16[8,8,257,1]{2,0,1,3:T(8,128)(2,1)S(1)} %fusion.19), kind=kOutput, calls=%fused_computation.39 | convolution fusion | flops 2631680 | bytes 2685056 | tf_op jit(solution)/shard_map/iht,ithd->ihd/dot_general | solution.py:87
  105.9 0.1 reshape.103
  106.0 1.9 %fusion.44 = (f32[8]{0:T(128)S(1)}, f32[8,1280]{1,0:T(8,128)S(1)}) fusion(bf16[8,640]{1,0:T(8,128)(2,1)S(1)} %reshape.103, bf16[1,640,1280]{2,1,0:T(8,128)(2,1)} %param.25, f32[1280]{0:T(1024)S(1)} %get-tuple-element.144), kind=kOutput, calls=%fused_computation.69 | convolution fusion | flops 13127672 | bytes 1694752 | tf_op jit(solution)/shard_map/dot_general | solution.py:89
  107.9 0.2 multiply_reduce_fusion.1
  108.1 0.0 copy-done
  108.1 0.0 copy-done.3
  108.1 0.9 fusion.45
  109.0 0.2 exponential_reduce_fusion
  109.3 0.1 subtract_subtract_fusion
  109.3 20.5 %all-gather = f32[128,1000]{1,0:T(8,128)S(1)} all-gather(f32[8,1000]{1,0:T(8,128)S(1)} %subtract_subtract_fusion), channel_id=2, replica_groups=mesh['group'=2,'sample'=16] {'sample'}, dimensions={0}, use_global_device_ids=true | all-gather | bytes 544000 | tf_op jit(solution)/shard_map/all_gather | solution.py:15
  129.8 0.8 while.18
  130.7 0.6 add_add_fusion
  (24 shorter events, 0.5 us)
Async XLA Ops:
  6.5 101.6 %copy-start = (bf16[1,1280,1000]{1,2,0:T(8,128)(2,1)S(1)}, bf16[1,1280,1000]{1,2,0:T(8,128)(2,1)}, u32[]{:S(2)}) copy-start(bf16[1,1280,1000]{1,2,0:T(8,128)(2,1)} %param.28) | copy-start | bytes 7680004
  6.5 12.2 %copy-start.2 = (bf16[1,257,1280]{2,1,0:T(8,128)(2,1)S(1)}, bf16[1,257,1280]{2,1,0:T(8,128)(2,1)}, u32[]{:S(2)}) copy-start(bf16[1,257,1280]{2,1,0:T(8,128)(2,1)} %param.19) | copy-start | bytes 1973764
  6.5 49.4 %all-gather.3.cloned.1.call-start = ((), (), s32[]{:S(2)}) async-start(), calls=%async_computation | async-start | bytes 2785280 | tf_op jit(solution)/shard_map/all_gather | solution.py:66
  55.9 7.3 %copy-start.1 = (f32[256,1280]{1,0:T(8,128)S(1)}, f32[256,1280]{1,0:T(8,128)}, u32[]{:S(2)}) copy-start(f32[256,1280]{1,0:T(8,128)} %bitcast_convert_fusion) | copy-start | bytes 3932164
  64.9 2.6 %copy-start.4 = (bf16[1,1280,640]{2,1,0:T(8,128)(2,1)S(1)}, bf16[1,1280,640]{2,1,0:T(8,128)(2,1)}, u32[]{:S(2)}) copy-start(bf16[1,1280,640]{2,1,0:T(8,128)(2,1)} %param.24) | copy-start | bytes 4915204
  64.9 2.6 %copy-start.5 = (bf16[1,1280,640]{2,1,0:T(8,128)(2,1)S(1)}, bf16[1,1280,640]{2,1,0:T(8,128)(2,1)}, u32[]{:S(2)}) copy-start(bf16[1,1280,640]{2,1,0:T(8,128)(2,1)} %param.23) | copy-start | bytes 4915204
  102.3 5.8 %copy-start.3 = (f32[1,1000]{1,0:T(1,128)S(1)}, f32[1,1000]{1,0:T(1,128)}, u32[]{:S(2)}) copy-start(f32[1,1000]{1,0:T(1,128)} %param.29) | copy-start | bytes 12004
Sparse Core Ops, SparseCore 0:
  9.5 46.3 all-gather.2
where the time goes:
time: 139 us; the launch traced here: 138 us
  waiting for transfers between devices  36.6 us (26%)
  matrix products  33.5 us (24%)
  blocking collectives  20.5 us (15%)
  local copies, waits for them, and re-layouts  16.8 us (12%)
  other arithmetic  15.4 us (11%)
  between operations  14.9 us (11%)
    all_gather x1, waiting for transfers between devices, shards(): portion = lax.all_gather(patches, 'sample', axis=1, tiled=True)  35.9 us
    all_gather x1, blocking collectives, combined_all(): gathered = jax.tree.map(lambda a: lax.all_gather(a, axis), part)  20.5 us
    dot_general x1, matrix products, shards(): jnp.einsum('hd,ithd->iht', query, key_rows, preferred_element_type=jnp.fl...  8.3 us
    reshape x1, local copies, waits for them, and re-layouts, shards(): full_rows[:, :, :inner].reshape(image_count, -1, head_count, HEAD_DIM)  7.9 us
    dot_general x1, matrix products, shards(): jnp.dot(flat, embed_weight, preferred_element_type=jnp.float32)  7.28 us
    dot_general x1, matrix products, shards(): jnp.dot(normed.reshape(-1, width), pair_weight, preferred_element_type=jn...  7.22 us
    reshape x1, local copies, waits for them, and re-layouts, shards(): full_rows[:, :, inner:].reshape(image_count, -1, head_count, HEAD_DIM)  5.74 us
    dot_general x1, matrix products, shards(): jnp.einsum('iht,ithd->ihd', attention, value_rows, preferred_element_type...  3.56 us
  transfers between devices with their start and end apart: 1, of which 1 were waited for; matrix products, arithmetic and copies ran while one was open for 8% of the time, Pallas kernels for 0%

commit v1 on v0

--- a/solution.py
+++ b/solution.py
@@ -1,8 +1,11 @@
+import functools
 import math
 
 import jax
 import jax.numpy as jnp
 from jax import lax
+from jax.experimental import pallas as pl
+from jax.experimental.pallas import tpu as pltpu
 from jax.sharding import PartitionSpec as P
 
 HEAD_DIM = 80
@@ -101,6 +104,385 @@
     return peak + jnp.log(total) - math.log(count)
 
 
+MESH = pl.DeviceIdType.MESH
+PLANE = 4
+BF16_ROWS = 16
+LOWEST = -1e30
+
+
+def flipped(index, turn, bits):
+    out = 0
+    for bit in range(bits):
+        step = 1 << bit
+        out = out + step * ((index // step + turn // step) % 2)
+    return out
+
+
+def split_in_two(values):
+    high = values.astype(jnp.bfloat16)
+    low = (values - high.astype(jnp.float32)).astype(jnp.bfloat16)
+    return jnp.concatenate([high, low], axis=0)
+
+
+def whole_kernel(
+    count,
+    heads,
+    patches,
+    cls_token,
+    ln1_gain,
+    ln1_bias,
+    lnf_gain,
+    lnf_bias,
+    head_bias,
+    patch_weight,
+    pos_embed,
+    w_query,
+    w_key,
+    w_value,
+    w_out,
+    head_w,
+    out,
+    embed,
+    position,
+    query_w,
+    key_w,
+    value_w,
+    out_w,
+    class_w,
+    place,
+    slots,
+    tokens,
+    normed,
+    probe,
+    gathered,
+    peak,
+    total,
+    part,
+    from_pair,
+    ring,
+    result,
+    load_sem,
+    recv_sem,
+    line_sem,
+    across_sem,
+    pair_sem,
+    relay_sem,
+    tail_send,
+    tail_recv,
+    spread_sem,
+):
+    me = lax.axis_index("sample")
+    core = me % 2
+    chip = me // 2
+    chips = count // 2
+    planes = count // PLANE
+    bits = planes.bit_length() - 1
+    plane = me // PLANE
+    spot = me % PLANE
+    beside = plane * PLANE + (spot + 2) % PLANE
+    twin = me + 1 - 2 * core
+    images, rows, depth = patches.shape
+    width = embed.shape[1]
+    inner = query_w.shape[1]
+    head_dim = inner // heads
+    pairs = heads * images
+
+    loads = []
+    for index, (source, target) in enumerate(
+        (
+            (pos_embed, position),
+            (w_query, query_w),
+            (w_key, key_w),
+            (patch_weight, embed),
+            (w_value, value_w),
+            (w_out, out_w),
+            (head_w, class_w),
+        )
+    ):
+        load = pltpu.make_async_copy(source.at[0], target, load_sem.at[index])
+        load.start()
+        loads.append(load)
+
+    barrier = pltpu.get_barrier_semaphore()
+    for step in range(1, chips):
+        pl.semaphore_signal(
+            barrier,
+            inc=1,
+            device_id={"sample": 2 * ((chip + step) % chips) + core},
+            device_id_type=MESH,
+        )
+    pl.semaphore_signal(barrier, inc=1, device_id={"sample": twin}, device_id_type=MESH)
+    pl.semaphore_wait(barrier, chips)
+
+    def send(source, origin, target, sem):
+        return pltpu.make_async_remote_copy(
+            src_ref=source,
+            dst_ref=slots.at[origin],
+            send_sem=sem,
+            recv_sem=recv_sem.at[origin],
+            device_id={"sample": target},
+            device_id_type=MESH,
+        )
+
+    def along(turn):
+        return flipped(plane, turn, bits) * PLANE + spot
+
+    def across(turn):
+        return flipped(plane, turn, bits) * PLANE + (spot + 2) % PLANE
+
+    def other(turn):
+        return flipped(plane, turn, bits) * PLANE + spot + 1 - 2 * core
+
+    def other_across(turn):
+        return flipped(plane, turn, bits) * PLANE + (spot + 2) % PLANE + 1 - 2 * core
+
+    def arrived(origin):
+        send(slots.at[origin], origin, twin, relay_sem.at[0]).wait_recv()
+
+    send(patches, me, beside, across_sem.at[0]).start()
+    for turn in range(1, planes):
+        send(patches, me, along(turn), line_sem.at[turn]).start()
+    send(patches, me, twin, pair_sem.at[0]).start()
+    slots[me] = patches[...]
+
+    loads[0].wait()
+    place[...] = position[...].astype(jnp.float32)[1:]
+    leading = cls_token[...].astype(jnp.float32) + position[0:1, :].astype(jnp.float32)
+    gain = ln1_gain[...]
+    bias = ln1_bias[...]
+    lead = jnp.broadcast_to(layer_norm(leading, gain, bias), (BF16_ROWS, width)).astype(jnp.bfloat16)
+    loads[1].wait()
+    query = jnp.dot(lead, query_w[...], preferred_element_type=jnp.float32)[:1]
+    row_head = lax.broadcasted_iota(jnp.int32, (pairs, inner), 0) // images
+    column = lax.broadcasted_iota(jnp.int32, (pairs, inner), 1)
+    own_head = (column >= row_head * head_dim) & (column < (row_head + 1) * head_dim)
+    spread = jnp.where(own_head, jnp.broadcast_to(query, (pairs, inner)), 0.0).astype(jnp.bfloat16)
+    loads[2].wait()
+    turned = lax.dot_general(
+        spread, key_w[...], (((1,), (1,)), ((), ())), preferred_element_type=jnp.float32
+    ) * (1.0 / math.sqrt(head_dim))
+    probe[...] = split_in_two(turned)
+    lead_row = lead[:1].astype(jnp.float32)
+    first = jnp.sum(turned * lead_row, axis=1, keepdims=True)
+    peak[...] = jnp.broadcast_to(first, peak.shape)
+    total[...] = jnp.ones(total.shape, jnp.float32)
+    gathered[...] = jnp.broadcast_to(lead_row, gathered.shape)
+    loads[3].wait()
+
+    span = PLANE * images * rows
+    token_image = (lax.broadcasted_iota(jnp.int32, (pairs, span), 1) // rows) % images
+    row_image = lax.broadcasted_iota(jnp.int32, (pairs, span), 0) % images
+    same = token_image == row_image
+
+    def turn_step(turn, carry):
+        @pl.when(turn < planes)
+        def _():
+            origin = along(turn)
+            arrived(origin)
+            send(slots.at[origin], origin, beside, across_sem.at[turn]).start()
+            send(slots.at[origin], origin, twin, pair_sem.at[turn]).start()
+
+        done = turn - 1
+        origin = across(done)
+        arrived(origin)
+        send(slots.at[origin], origin, twin, relay_sem.at[done]).start()
+        arrived(other(done))
+        arrived(other_across(done))
+
+        where = flipped(plane, done, bits)
+        block = slots[pl.ds(where * PLANE, PLANE)].reshape(span, depth)
+        tokens[...] = jnp.dot(block, embed[...], preferred_element_type=jnp.float32)
+        for one in range(PLANE):
+            low = one * images * rows
+            start = pl.multiple_of((where * PLANE + one) * rows, rows)
+            spots = place[pl.ds(start, rows), :]
+            value = tokens[low : low + images * rows, :].reshape(images, rows, width) + spots[None]
+            value = layer_norm(value, gain[None], bias[None])
+            normed[low : low + images * rows, :] = value.reshape(images * rows, width).astype(
+                jnp.bfloat16
+            )
+        scores = lax.dot_general(
+            probe[...], normed[...], (((1,), (1,)), ((), ())), preferred_element_type=jnp.float32
+        )
+        scores = jnp.where(same, scores[:pairs] + scores[pairs:], LOWEST)
+        before = peak[:, :1]
+        now = jnp.maximum(before, jnp.max(scores, axis=1, keepdims=True))
+        shrink = jnp.exp(before - now)
+        chance = jnp.where(same, jnp.exp(scores - now), 0.0)
+        peak[...] = jnp.broadcast_to(now, peak.shape)
+        total[...] = total[...] * shrink + jnp.sum(chance, axis=1, keepdims=True)
+        gathered[...] = gathered[...] * shrink + jnp.dot(
+            chance.astype(jnp.bfloat16), normed[...], preferred_element_type=jnp.float32
+        )
+        return carry
+
+    lax.fori_loop(1, planes + 1, turn_step, 0)
+
+    loads[4].wait()
+    pooled = gathered[...] / total[:, :1]
+    values = jnp.dot(split_in_two(pooled), value_w[...], preferred_element_type=jnp.float32)
+    values = jnp.where(own_head, values[:pairs] + values[pairs:], 0.0)
+    mixed = jnp.sum(values.reshape(heads, images, inner), axis=0).astype(jnp.bfloat16)
+    loads[5].wait()
+    hidden = leading + jnp.dot(mixed, out_w[...], preferred_element_type=jnp.float32)
+    final = layer_norm(hidden, lnf_gain[...], lnf_bias[...]).astype(jnp.bfloat16)
+    loads[6].wait()
+    logits = jnp.dot(final, class_w[...], preferred_element_type=jnp.float32) + head_bias[...]
+    lifted = logits - jnp.max(logits, axis=-1, keepdims=True)
+    logp = lifted - jnp.log(jnp.sum(jnp.exp(lifted), axis=-1, keepdims=True))
+
+    half = part.shape[2]
+    classes = out.shape[1]
+    part[0] = logp[:, :half]
+    part[1] = jnp.concatenate(
+        [logp[:, half:], jnp.zeros((images, 2 * half - classes), jnp.float32)], axis=1
+    )
+    swap = pltpu.make_async_remote_copy(
+        src_ref=part.at[1 - core],
+        dst_ref=from_pair,
+        send_sem=tail_send.at[0],
+        recv_sem=tail_recv.at[0],
+        device_id={"sample": twin},
+        device_id_type=MESH,
+    )
+    swap.start()
+    swap.wait_recv()
+    mine = part[core]
+    theirs = from_pair[...]
+    high = jnp.maximum(mine, theirs)
+    ring[chip] = high + jnp.log(jnp.exp(mine - high) + jnp.exp(theirs - high))
+
+    def pass_on(origin, target, step):
+        return pltpu.make_async_remote_copy(
+            src_ref=ring.at[origin],
+            dst_ref=ring.at[origin],
+            send_sem=spread_sem.at[step],
+            recv_sem=tail_recv.at[2 + origin],
+            device_id={"sample": target},
+            device_id_type=MESH,
+        )
+
+    for step in range(1, chips):
+        pass_on(chip, 2 * ((chip + step) % chips) + core, step).start()
+    for step in range(1, chips):
+        pass_on((chip + step) % chips, me, step).wait_recv()
+    every = ring[...]
+    high = jnp.max(every, axis=0)
+    result[core] = high + jnp.log(jnp.sum(jnp.exp(every - high[None]), axis=0)) - math.log(count)
+    share = pltpu.make_async_remote_copy(
+        src_ref=result.at[core],
+        dst_ref=result.at[core],
+        send_sem=tail_send.at[1],
+        recv_sem=tail_recv.at[1],
+        device_id={"sample": twin},
+        device_id_type=MESH,
+    )
+    share.start()
+    for turn in range(planes):
+        send(patches, me, beside, across_sem.at[turn]).wait_send()
+        send(patches, me, twin, pair_sem.at[turn]).wait_send()
+        send(patches, me, twin, relay_sem.at[turn]).wait_send()
+        if turn:
+            send(patches, me, twin, line_sem.at[turn]).wait_send()
+    swap.wait_send()
+    for step in range(1, chips):
+        pass_on(chip, twin, step).wait_send()
+    pltpu.make_async_remote_copy(
+        src_ref=result.at[core],
+        dst_ref=result.at[1 - core],
+        send_sem=tail_send.at[1],
+        recv_sem=tail_recv.at[1],
+        device_id={"sample": twin},
+        device_id_type=MESH,
+    ).wait_recv()
+    share.wait_send()
+    out[:, :half] = result[0]
+    out[:, half:] = result[1][:, : classes - half]
+
+
+def kernel_shards(
+    patches,
+    patch_weight,
+    cls_token,
+    pos_embed,
+    ln1_gain,
+    ln1_bias,
+    w_query,
+    w_key,
+    w_value,
+    w_out,
+    lnf_gain,
+    lnf_bias,
+    head_w,
+    head_bias,
+):
+    count = lax.axis_size("sample")
+    images, rows, depth = patches.shape
+    width = patch_weight.shape[2]
+    inner = w_query.shape[2]
+    heads = inner // HEAD_DIM
+    pairs = heads * images
+    planes = count // PLANE
+    chips = count // 2
+    classes = head_w.shape[2]
+    half = pl.cdiv(classes, 256) * 128
+    span = PLANE * images * rows
+    near = pl.BlockSpec(memory_space=pltpu.VMEM)
+    far = pl.BlockSpec(memory_space=pl.ANY)
+    dma = pltpu.SemaphoreType.DMA
+    f32, bf16 = jnp.float32, jnp.bfloat16
+    large = (patch_weight, pos_embed, w_query, w_key, w_value, w_out, head_w)
+    embed, position, query_w, key_w, value_w, out_w, class_w = (
+        pltpu.VMEM(a.shape[1:], a.dtype) for a in large
+    )
+    return pl.pallas_call(
+        functools.partial(whole_kernel, count, heads),
+        out_shape=jax.ShapeDtypeStruct((images, classes), f32),
+        in_specs=[near] * 7 + [far] * 7,
+        out_specs=near,
+        scratch_shapes=[
+            embed,
+            position,
+            query_w,
+            key_w,
+            value_w,
+            out_w,
+            class_w,
+            pltpu.VMEM((rows * count, width), f32),
+            pltpu.VMEM((count, images, rows, depth), bf16),
+            pltpu.VMEM((span, width), f32),
+            pltpu.VMEM((span, width), bf16),
+            pltpu.VMEM((2 * pairs, width), bf16),
+            pltpu.VMEM((pairs, width), f32),
+            pltpu.VMEM((pairs, 128), f32),
+            pltpu.VMEM((pairs, 128), f32),
+            pltpu.VMEM((2, images, half), f32),
+            pltpu.VMEM((images, half), f32),
+            pltpu.VMEM((chips, images, half), f32),
+            pltpu.VMEM((2, images, half), f32),
+            dma((7,)),
+            dma((count,)),
+            dma((planes,)),
+            dma((planes,)),
+            dma((planes,)),
+            dma((planes,)),
+            dma((2,)),
+            dma((2 + chips,)),
+            dma((chips,)),
+        ],
+        compiler_params=pltpu.CompilerParams(
+            collective_id=0, has_side_effects=True, vmem_limit_bytes=60 << 20
+        ),
+    )(patches, cls_token, ln1_gain, ln1_bias, lnf_gain, lnf_bias, head_bias, *large)
+
+
+def takes_kernel(mesh, patches):
+    count = mesh.shape["sample"]
+    planes = count // PLANE
+    rows = patches.shape[1] // count
+    return count % PLANE == 0 and planes & (planes - 1) == 0 and rows % BF16_ROWS == 0
+
+
 def solution(mesh):
     placed = (
         P("group", "sample", None),
@@ -118,6 +500,11 @@
         P("sample", None, None),
         P("sample", None),
     )
-    return jax.shard_map(
-        shards, mesh=mesh, in_specs=placed, out_specs=P("group", None), check_vma=False
-    )
+
+    def run(*arrays):
+        step = kernel_shards if takes_kernel(mesh, arrays[0]) else shards
+        return jax.shard_map(
+            step, mesh=mesh, in_specs=placed, out_specs=P("group", None), check_vma=False
+        )(*arrays)
+
+    return run

time: 139 us -> 48.1 us (0.35)
  Pallas kernels: 0 us -> 41.9 us
  waiting for transfers between devices: 36.6 us -> 0 us
  matrix products: 33.5 us -> 0 us
  blocking collectives: 20.5 us -> 0 us
  other arithmetic: 15.4 us -> 0 us
  between operations: 14.9 us -> 0.01 us
  local copies, waits for them, and re-layouts: 16.8 us -> 5.9 us
    pallas_call x0 -> x1, Pallas kernels: none -> 41.9 us  [kernel_shards(): pl.pallas_call(functools.partial(whole_kernel, count, heads), out_shape=j...]
    all_gather x1 -> x0, waiting for transfers between devices: 35.9 us -> none  [shards(): portion = lax.all_gather(patches, 'sample', axis=1, tiled=True)]
    dot_general x8 -> x0, matrix products: 33.5 us -> none  [the longest x1 8.3 us: shards(): jnp.einsum('hd,ithd->iht', query, key_rows, preferred_element_type=jnp.fl...]
    all_gather x1 -> x0, blocking collectives: 20.5 us -> none  [combined_all(): gathered = jax.tree.map(lambda a: lax.all_gather(a, axis), part)]
    reshape x5 -> x0, local copies, waits for them, and re-layouts: 16.8 us -> none  [the longest x1 7.9 us: shards(): full_rows[:, :, :inner].reshape(image_count, -1, head_count, HEAD_DIM)]
    unnamed x12 -> x2, local copies, waits for them, and re-layouts: 0.03 us -> 5.9 us
    convert_element_type x3 -> x0, other arithmetic: 3.27 us -> none  [the longest x1 2.52 us: shards(): normed = layer_norm(tokens, gain_first, bias_first).astype(jnp.bfloat16)]
    reduce_sum x5 -> x0, other arithmetic: 3.25 us -> none  [the longest x3 2.44 us: layer_norm(): spread = jnp.mean(center * center, axis=-1, keepdims=True)]
  transfers between devices with their start and end apart: 1 -> 0, of which waited for: 1 -> 0; matrix products, arithmetic and copies ran while one was open for 8% -> 0% of each run, Pallas kernels for 0% -> 0%
where the time goes in v1:
time: 48.1 us; the launch traced here: 47.8 us
  Pallas kernels  41.9 us (87%)
  local copies, waits for them, and re-layouts  5.9 us (12%)
    pallas_call x1, Pallas kernels, kernel_shards(): pl.pallas_call(functools.partial(whole_kernel, count, heads), out_shape=j...  41.9 us
    unnamed x2, local copies, waits for them, and re-layouts  5.9 us

profile of v1, /device:TPU:0, one launch (start us, length us, event | category | flops | bytes accessed | tf_op | source)
XLA Modules:
  0.0 47.8 jit_solution(5568698664456504708)
XLA Ops:
  0.0 4.5 %copy.15.head_w = bf16[1,1280,1000]{2,1,0:T(8,128)(2,1)} copy(bf16[1,1280,1000]{1,2,0:T(8,128)(2,1)} %param.26) | data formatting | bytes 5120000 | tf_op args[12]
  4.5 41.9 %shard_map.136 = f32[8,1000]{1,0:T(8,128)} custom-call(bf16[8,16,588]{2,1,0:T(8,128)(2,1)} %patches.1, bf16[1,1280]{1,0:T(2,128)(2,1)} %cls_token.1, f32[1,1280]{1,0:T(1,128)} %ln1_gain.1, f32[1,1280]{1,0:T(1,128)} %ln1_bias.1, f32[1,1280]{1,0:T(1,128)} %lnf_gain.1, f32[1,1280]{1,0:T(1,128)} %lnf_bias.1, f32[1,1000]{1,0:T(1,128)} %head_bias.1, ...), custom_call_target="tpu_custom_call" | custom-call | tf_op jit(solution)/shard_map/pallas_call | solution.py:438
  46.5 1.4 %copy.17 = f32[8,1000]{1,0:T(8,128)} copy(f32[8,1000]{1,0:T(8,128)} %shard_map.136) | data formatting | bytes 64000
